TPU v7x, 512 devices: a whole 4x4x16 slice. The times are simulated.
512 devices in a mesh: tile: 16 (over y, x), depth: 32 (over z, core).
Axes of the slice: x: 4, y: 4, z: 16, core: 2. Of those that a mesh axis runs over, the one named last changes fastest.
Arguments:
- patches: float32 [1024, 256, 256], P('tile', 'depth'), may hold values from -6 to 6
- patch_owner: int32 [1024, 1], P('tile'), may hold values from 0 to 15; in each aligned block of 64 rows (0 to 63, 64 to 127, ...) at most 8 rows name the same one
- patch_level: int32 [1024], P('tile'), may hold values from 0 to 63
- phases: float32 [1024, 256, 256], P('tile', None, 'depth'), may hold values from -3.140625 to 3.140625
Outputs:
- intensity: float32 [1024, 256, 256], P('tile', 'depth')
Inputs may be any that keep to these rules, and one draw needn't show every extreme that they name: `patch_owner`: among the 64 patches of one index of tile, at most 8 have the same owner.
All inputs are finite; a program needn't handle non-finite values.
Results may differ from a plain program's by a relative error of at most 0.00017.
Values sent between devices are 32-bit elements; how exact they have to be, the bound alone decides.
A program may use at most 64 MiB of HBM per device.

v0:
```python
import math
import jax
import jax.numpy as jnp
from jax import lax
from jax.sharding import PartitionSpec as P

HIGHEST_PRECISION = lax.Precision.HIGHEST


def sent_together(arrays, axis, split_dim, concat_dim, along):
    widths = [a.shape[along] for a in arrays]
    both = jnp.concatenate(arrays, axis=along)
    filled = lax.all_to_all(both, axis, split_axis=split_dim, concat_axis=concat_dim, tiled=True)
    return tuple(jnp.split(filled, [sum(widths[:k]) for k in range(1, len(widths))], axis=along))


def tables(extent):
    indices = jnp.arange(extent, dtype=jnp.int32)
    product = indices[:, None] * indices[None, :] % extent
    angles = product.astype(jnp.float32) * (2.0 * math.pi / extent)
    return (jnp.cos(angles), jnp.sin(angles))


def right_apply(values, matrix):
    return jnp.einsum(
        "src,ck->srk",
        values,
        matrix,
        precision=HIGHEST_PRECISION,
        preferred_element_type=jnp.float32,
    )


def apply_rows(matrix, values):
    return jnp.einsum(
        "jk,skc->sjc",
        matrix,
        values,
        precision=HIGHEST_PRECISION,
        preferred_element_type=jnp.float32,
    )


def refocus(field, real_gain, imag_gain):
    extent = field.shape[2]
    cosine_table, sine_table = tables(extent)
    col_real = right_apply(field, cosine_table)
    col_imag = -right_apply(field, sine_table)
    col_real, col_imag = sent_together((col_real, col_imag), "depth", 2, 1, 0)
    spec_real = apply_rows(cosine_table, col_real) + apply_rows(sine_table, col_imag)
    spec_imag = apply_rows(cosine_table, col_imag) - apply_rows(sine_table, col_real)
    prop_real = spec_real * real_gain - spec_imag * imag_gain
    prop_imag = spec_real * imag_gain + spec_imag * real_gain
    back_real = apply_rows(cosine_table, prop_real) - apply_rows(sine_table, prop_imag)
    back_imag = apply_rows(cosine_table, prop_imag) + apply_rows(sine_table, prop_real)
    back_real, back_imag = sent_together((back_real, back_imag), "depth", 1, 2, 0)
    field_real = right_apply(back_real, cosine_table) - right_apply(back_imag, sine_table)
    field_imag = right_apply(back_real, sine_table) + right_apply(back_imag, cosine_table)
    return (field_real * field_real + field_imag * field_imag) * (1.0 / float(extent) ** 4)


def select_gains(selector, phase_block, lead):
    flattened = phase_block.reshape(phase_block.shape[0], -1)
    real_gain = jnp.dot(
        selector,
        jnp.cos(flattened),
        precision=HIGHEST_PRECISION,
        preferred_element_type=jnp.float32,
    )
    imag_gain = jnp.dot(
        selector,
        jnp.sin(flattened),
        precision=HIGHEST_PRECISION,
        preferred_element_type=jnp.float32,
    )
    shape_out = (lead, phase_block.shape[1], phase_block.shape[2])
    return (real_gain.reshape(shape_out), imag_gain.reshape(shape_out))


def on_device(patches, patch_owner, patch_level, phases):
    patch_count, row_count, extent = patches.shape
    levels = phases.shape[0]
    owners = lax.axis_size("tile")
    owner_column = patch_owner[:, 0]
    gathered = lax.all_gather(phases, "tile", axis=0, tiled=True)
    depth_index = owner_column * levels + patch_level
    depth_hot = (
        depth_index[:, None] == jnp.arange(owners * levels, dtype=jnp.int32)[None, :]
    ).astype(jnp.float32)
    real_gain, imag_gain = select_gains(depth_hot, gathered, patch_count)
    return refocus(patches, real_gain, imag_gain)


def solution(mesh):
    return jax.shard_map(
        on_device,
        mesh=mesh,
        in_specs=(P("tile", "depth", None), P("tile", None), P("tile"), P("tile", None, "depth")),
        out_specs=P("tile", "depth", None),
        check_vma=False,
    )
```

profile of v0, /device:TPU:1, one launch (start us, length us, event | category | flops | bytes accessed | tf_op | source)
XLA Modules:
  0.0 253.1 jit_solution(1416911551636459273)
XLA Ops:
  6.5 0.7 all-gather.2.cloned.1.call-update
  7.3 0.3 copy-done
  7.6 1.6 fusion.4
  9.2 1.6 convolution_bitcast_fusion
  10.9 1.4 copy.66
  12.3 17.0 %all-to-all-start = ((f32[128,8,256]{0,1,2:T(8,128)}), f32[128,8,256]{0,1,2:T(8,128)S(1)}, u32[]{:S(2)}, u32[]{:S(2)}) async-start(f32[128,8,256]{0,1,2:T(8,128)} %copy.66), calls=%async_computation | async-start | bytes 2097152 | tf_op jit(solution)/shard_map/all_to_all | solution.py:13
  29.4 55.5 %all-to-all-done = f32[128,8,256]{0,1,2:T(8,128)S(1)} async-done(((f32[128,8,256]{0,1,2:T(8,128)}), f32[128,8,256]{0,1,2:T(8,128)S(1)}, u32[]{:S(2)}, u32[]{:S(2)}) %all-to-all-start) | async-done | bytes 1048608 | tf_op jit(solution)/shard_map/all_to_all | solution.py:13
  85.1 0.3 fusion.119
  85.6 0.5 copy.69
  86.2 0.5 copy.71
  86.7 1.6 fusion.35
  88.2 2.4 fusion.33
  90.6 1.6 fusion.12
  92.1 9.5 %all-gather.2.cloned.1.call-done = f32[1024,256,8]{1,2,0:T(8,128)} async-done(((f32[64,256,8]{1,2,0:T(8,128)}), f32[1024,256,8]{1,2,0:T(8,128)}) %all-gather.2.cloned.1.call-update) | async-done | bytes 8388624 | tf_op jit(solution)/shard_map/all_gather | solution.py:85
  101.7 8.8 %copy.72 = f32[1024,256,8]{0,2,1:T(8,128)} copy(f32[1024,256,8]{1,2,0:T(8,128)} %all-gather.2.cloned.1.call-done) | data formatting | bytes 16777216 | tf_op jit(solution)/shard_map/all_gather | solution.py:85
  110.5 30.3 %cosine_bitcast_fusion = (f32[256,8,1024]{2,1,0:T(8,128)S(1)}, f32[256,8,1024]{2,1,0:T(8,128)S(1)}) fusion(f32[1024,256,8]{0,2,1:T(8,128)} %copy.72), kind=kLoop, calls=%fused_computation.5 | loop fusion | bytes 25165824 | tf_op jit(solution)/shard_map/dot_general | solution.py:64
  140.8 9.3 %fusion.2 = f32[64,256,8]{1,0,2:T(8,128)S(1)} fusion(f32[256,8,1024]{2,1,0:T(8,128)S(1)} %get-tuple-element.5, s32[64]{0:T(128)S(1)} %bitcast_add_fusion), kind=kOutput, calls=%fused_computation.2 | convolution fusion | flops 1610678272 | bytes 8913152 | tf_op jit(solution)/shard_map/dot_general | solution.py:64
  150.1 9.7 %fusion = f32[64,256,8]{1,0,2:T(8,128)S(1)} fusion(f32[256,8,1024]{2,1,0:T(8,128)S(1)} %get-tuple-element.6, s32[64]{0:T(128)S(1)} %bitcast_add_fusion), kind=kOutput, calls=%fused_computation | convolution fusion | flops 1610678272 | bytes 8913152 | tf_op jit(solution)/shard_map/dot_general | solution.py:70
  159.9 2.0 multiply_subtract_fusion
  161.9 1.6 fusion.31
  163.5 1.6 fusion.29
  165.0 1.7 fusion.10
  166.8 1.6 fusion.9
  168.4 0.6 copy.82
  169.0 68.6 %all_to_all.30 = f32[128,256,8]{0,2,1:T(8,128)S(1)} all-to-all(f32[128,256,8]{0,2,1:T(8,128)S(1)} %copy.82), channel_id=1, replica_groups=mesh['tile'=16,'depth'=32] {'depth'}, dimensions={1} | all-to-all | bytes 2097152 | tf_op jit(solution)/shard_map/all_to_all | solution.py:13
  237.7 0.4 fusion.118
  238.2 0.4 copy.84
  238.6 1.6 fusion.18
  240.2 1.6 fusion.27
  241.8 0.4 copy.86
  242.1 1.6 fusion.8
  243.7 2.4 fusion.7
  (15 shorter events, 0.8 us)
Async XLA Ops:
  6.5 1.0 copy-start
  6.5 22.8 %copy-start.2 = (s32[64]{0:T(128)S(1)}, s32[64]{0:T(128)}, u32[]{:S(2)}) copy-start(s32[64]{0:T(128)} %param.6) | copy-start | bytes 772
  6.5 22.8 %copy-start.3 = (s32[64,1]{0,1:T(1,128)S(1)}, s32[64,1]{0,1:T(1,128)}, u32[]{:S(2)}) copy-start(s32[64,1]{0,1:T(1,128)} %param.5) | copy-start | bytes 772
  6.5 95.1 %all-gather.2.cloned.1.call-start = ((), (), s32[]{:S(2)}) async-start(), calls=%async_computation.2 | async-start | bytes 8912896 | tf_op jit(solution)/shard_map/all_gather | solution.py:85
  12.3 72.6 %all-to-all-start = ((f32[128,8,256]{0,1,2:T(8,128)}), f32[128,8,256]{0,1,2:T(8,128)S(1)}, u32[]{:S(2)}, u32[]{:S(2)}) async-start(f32[128,8,256]{0,1,2:T(8,128)} %copy.66), calls=%async_computation | async-start | bytes 2097152 | tf_op jit(solution)/shard_map/all_to_all | solution.py:13
  140.8 19.1 %copy-start.1 = (f32[64,8,256]{2,1,0:T(8,128)S(1)}, f32[64,8,256]{2,1,0:T(8,128)}, u32[]{:S(2)}) copy-start(f32[64,8,256]{2,1,0:T(8,128)} %fusion.33) | copy-start | bytes 1572868
Sparse Core Ops, SparseCore 0:
  10.3 91.2 all-gather.1
where the time goes:
time: 257 us; the launch traced here: 253 us
  blocking collectives  68.6 us (27%)
  waiting for transfers between devices  65.8 us (26%)
  local copies, waits for them, and re-layouts  44.4 us (17%)
  matrix products  43.2 us (17%)
  starting transfers between devices  17 us (7%)
  between operations  13.8 us (5%)
    all_to_all x1, blocking collectives, sent_together(): lax.all_to_all(both, axis, split_axis=split_dim, concat_axis=concat_dim,...  68.6 us
    all_to_all x1, waiting for transfers between devices, sent_together(): lax.all_to_all(both, axis, split_axis=split_dim, concat_axis=concat_dim,...  55.5 us
    dot_general x1, local copies, waits for them, and re-layouts, select_gains(): jnp.dot(selector, jnp.cos(flattened), precision=HIGHEST_PRECISION, prefer...  30.3 us
    all_to_all x1, starting transfers between devices, sent_together(): lax.all_to_all(both, axis, split_axis=split_dim, concat_axis=concat_dim,...  17 us
    dot_general x8, matrix products, apply_rows(): jnp.einsum('jk,skc->sjc', matrix, values, precision=HIGHEST_PRECISION, pr...  13.9 us
    dot_general x6, matrix products, right_apply(): jnp.einsum('src,ck->srk', values, matrix, precision=HIGHEST_PRECISION, pr...  10.3 us
    dot_general x1, matrix products, select_gains(): jnp.dot(selector, jnp.sin(flattened), precision=HIGHEST_PRECISION, prefer...  9.72 us
    all_gather x1, waiting for transfers between devices, on_device(): gathered = lax.all_gather(phases, 'tile', axis=0, tiled=True)  9.54 us
  transfers between devices with their start and end apart: 2, of which 2 were waited for; matrix products, arithmetic and copies ran while one was open for 5% of the time, Pallas kernels for 0%

commit v1 on v0

--- a/solution.py
+++ b/solution.py
@@ -5,6 +5,22 @@
 from jax.sharding import PartitionSpec as P
 
 HIGHEST_PRECISION = lax.Precision.HIGHEST
+
+
+def collect(x, axis, dim):
+    ways, here, step = (lax.axis_size(axis), lax.axis_index(axis), x.shape[dim])
+    dims = [n * ways if d == dim else n for d, n in enumerate(x.shape)]
+    full = lax.dynamic_update_slice_in_dim(jnp.zeros(dims, x.dtype), x, here * step, axis=dim)
+    going_up = going_down = x
+    for far in range(1, ways // 2 + 1):
+        going_up = lax.ppermute(going_up, axis, [(d, (d + 1) % ways) for d in range(ways)])
+        full = lax.dynamic_update_slice_in_dim(full, going_up, (here - far) % ways * step, axis=dim)
+        if 2 * far < ways:
+            going_down = lax.ppermute(going_down, axis, [(d, (d - 1) % ways) for d in range(ways)])
+            full = lax.dynamic_update_slice_in_dim(
+                full, going_down, (here + far) % ways * step, axis=dim
+            )
+    return full
 
 
 def sent_together(arrays, axis, split_dim, concat_dim, along):
@@ -82,7 +98,7 @@
     levels = phases.shape[0]
     owners = lax.axis_size("tile")
     owner_column = patch_owner[:, 0]
-    gathered = lax.all_gather(phases, "tile", axis=0, tiled=True)
+    gathered = collect(phases, "tile", 0)
     depth_index = owner_column * levels + patch_level
     depth_hot = (
         depth_index[:, None] == jnp.arange(owners * levels, dtype=jnp.int32)[None, :]

time: 257 us -> 755 us (2.94)
  the two profiles are of different devices: /device:TPU:1 before, /device:TPU:31 now
where the time goes in v1:
time: 755 us; the launch traced here: 747 us
  local copies, waits for them, and re-layouts  468 us (62%)
  starting transfers between devices  117 us (15%)
  blocking collectives  72.5 us (10%)
  matrix products  44.9 us (6%)
  waiting for transfers between devices  43.9 us (6%)
    dynamic_update_slice x8, local copies, waits for them, and re-layouts, collect(): lax.dynamic_update_slice_in_dim(full, going_up, (here - far) % ways * ste...  204 us
    dynamic_update_slice x7, local copies, waits for them, and re-layouts, collect(): lax.dynamic_update_slice_in_dim(full, going_down, (here + far) % ways * s...  163 us
    ppermute x8, starting transfers between devices, collect(): lax.ppermute(going_up, axis, [(d, (d + 1) % ways) for d in range(ways)])  85.9 us
    all_to_all x1, blocking collectives, sent_together(): lax.all_to_all(both, axis, split_axis=split_dim, concat_axis=concat_dim,...  72.5 us
    ppermute x8, waiting for transfers between devices, collect(): lax.ppermute(going_up, axis, [(d, (d + 1) % ways) for d in range(ways)])  43.9 us
    dynamic_update_slice x1, local copies, waits for them, and re-layouts, collect(): lax.dynamic_update_slice_in_dim(jnp.zeros(dims, x.dtype), x, here * step,...  42.7 us
    dot_general x1, local copies, waits for them, and re-layouts, select_gains(): jnp.dot(selector, jnp.cos(flattened), precision=HIGHEST_PRECISION, prefer...  30.5 us
    all_to_all x1, starting transfers between devices, sent_together(): lax.all_to_all(both, axis, split_axis=split_dim, concat_axis=concat_dim,...  15.9 us
  transfers between devices with their start and end apart: 16, of which 6 were waited for; matrix products, arithmetic and copies ran while one was open for 53% of the time, Pallas kernels for 0%

profile of v1, /device:TPU:31, one launch (start us, length us, event | category | flops | bytes accessed | tf_op | source)
XLA Modules:
  0.0 747.3 jit_solution(8789301310299569675)
XLA Ops:
  5.7 15.9 %all-to-all-start = ((f32[128,8,256]{0,1,2:T(8,128)}), f32[128,8,256]{0,1,2:T(8,128)S(1)}, u32[]{:S(2)}, u32[]{:S(2)}) async-start(f32[128,8,256]{0,1,2:T(8,128)} %copy.82), calls=%async_computation | async-start | bytes 2097152 | tf_op jit(solution)/shard_map/all_to_all | solution.py:29
  27.0 9.9 %collective-permute-done = f32[64,256,8]{1,2,0:T(8,128)} collective-permute-done((f32[64,256,8]{1,2,0:T(8,128)S(1)}, f32[64,256,8]{1,2,0:T(8,128)}, u32[]{:S(2)}, u32[]{:S(2)}) %collective-permute-start) | collective-permute-done | bytes 524320 | tf_op jit(solution)/shard_map/ppermute | solution.py:16
  44.3 8.7 %collective-permute-done.2 = f32[64,256,8]{1,2,0:T(8,128)} collective-permute-done((f32[64,256,8]{1,2,0:T(8,128)}, f32[64,256,8]{1,2,0:T(8,128)}, u32[]{:S(2)}, u32[]{:S(2)}) %collective-permute-start.2) | collective-permute-done | bytes 524320 | tf_op jit(solution)/shard_map/ppermute | solution.py:16
  53.0 7.4 collective-permute-start.4
  62.3 7.8 %collective-permute-done.4 = f32[64,256,8]{1,2,0:T(8,128)S(1)} collective-permute-done((f32[64,256,8]{1,2,0:T(8,128)}, f32[64,256,8]{1,2,0:T(8,128)S(1)}, u32[]{:S(2)}, u32[]{:S(2)}) %collective-permute-start.4) | collective-permute-done | bytes 524320 | tf_op jit(solution)/shard_map/ppermute | solution.py:16
  70.2 7.3 collective-permute-start.6
  79.4 6.7 collective-permute-done.6
  86.1 7.4 collective-permute-start.8
  95.5 5.8 collective-permute-done.8
  101.3 7.4 collective-permute-start.10
  115.6 7.5 %collective-permute-start.12 = (f32[64,256,8]{1,2,0:T(8,128)}, f32[64,256,8]{1,2,0:T(8,128)}, u32[]{:S(2)}, u32[]{:S(2)}) collective-permute-start(f32[64,256,8]{1,2,0:T(8,128)} %collective-permute-done.10), channel_id=1, source_target_pairs={{0,32},{32,64},{64,96},{96,128},{128,160},{160,192},{192,224},{224... | collective-permute-start | bytes 1572872 | tf_op jit(solution)/shard_map/ppermute | solution.py:16
  130.3 42.7 %dynamic_update_slice.48 = f32[1024,256,8]{0,2,1:T(8,128)} dynamic-update-slice(f32[1024,256,8]{0,2,1:T(8,128)} %broadcast_in_dim.2, f32[64,256,8]{0,2,1:T(8,128)S(1)} %copy.88, s32[]{:T(128)S(6)} %select_n.144, s32[]{:T(128)} %constant.105.clone.1, s32[]{:T(128)} %constant.105.clone.1) | dynamic-update-slice | bytes 1048580 | tf_op jit(solution)/shard_map/dynamic_update_slice | solution.py:13
  174.5 7.7 %dynamic_update_slice.49 = f32[1024,256,8]{0,2,1:T(8,128)} dynamic-update-slice(f32[1024,256,8]{0,2,1:T(8,128)} %dynamic_update_slice.48, f32[64,256,8]{0,2,1:T(8,128)S(1)} %copy.89, s32[]{:T(128)S(6)} %select_n.146, s32[]{:T(128)} %constant.105.clone.1, s32[]{:T(128)} %constant.105.clone.1) | dynamic-update-slice | bytes 1048580 | tf_op jit(solution)/shard_map/dynamic_update_slice | solution.py:17
  182.6 8.4 %dynamic_update_slice.50 = f32[1024,256,8]{0,2,1:T(8,128)} dynamic-update-slice(f32[1024,256,8]{0,2,1:T(8,128)} %dynamic_update_slice.49, f32[64,256,8]{0,2,1:T(8,128)S(1)} %copy.90, s32[]{:T(128)S(6)} %select_n.148, s32[]{:T(128)} %constant.105.clone.1, s32[]{:T(128)} %constant.105.clone.1) | dynamic-update-slice | bytes 1048580 | tf_op jit(solution)/shard_map/dynamic_update_slice | solution.py:20
  192.5 42.9 %dynamic_update_slice.51 = f32[1024,256,8]{0,2,1:T(8,128)} dynamic-update-slice(f32[1024,256,8]{0,2,1:T(8,128)} %dynamic_update_slice.50, f32[64,256,8]{0,2,1:T(8,128)S(1)} %copy.91, s32[]{:T(128)S(6)} %select_n.150, s32[]{:T(128)} %constant.105.clone.1, s32[]{:T(128)} %constant.105.clone.1) | dynamic-update-slice | bytes 1048580 | tf_op jit(solution)/shard_map/dynamic_update_slice | solution.py:17
  236.9 42.9 %dynamic_update_slice.52 = f32[1024,256,8]{0,2,1:T(8,128)} dynamic-update-slice(f32[1024,256,8]{0,2,1:T(8,128)} %dynamic_update_slice.51, f32[64,256,8]{0,2,1:T(8,128)S(1)} %copy.92, s32[]{:T(128)S(6)} %select_n.152, s32[]{:T(128)} %constant.105.clone.1, s32[]{:T(128)} %constant.105.clone.1) | dynamic-update-slice | bytes 1048580 | tf_op jit(solution)/shard_map/dynamic_update_slice | solution.py:20
  280.3 8.4 %dynamic_update_slice.53 = f32[1024,256,8]{0,2,1:T(8,128)} dynamic-update-slice(f32[1024,256,8]{0,2,1:T(8,128)} %dynamic_update_slice.52, f32[64,256,8]{0,2,1:T(8,128)S(1)} %copy.93, s32[]{:T(128)S(6)} %select_n.154, s32[]{:T(128)} %constant.105.clone.1, s32[]{:T(128)} %constant.105.clone.1) | dynamic-update-slice | bytes 1048580 | tf_op jit(solution)/shard_map/dynamic_update_slice | solution.py:17
  290.2 8.4 %dynamic_update_slice.54 = f32[1024,256,8]{0,2,1:T(8,128)} dynamic-update-slice(f32[1024,256,8]{0,2,1:T(8,128)} %dynamic_update_slice.53, f32[64,256,8]{0,2,1:T(8,128)S(1)} %copy.94, s32[]{:T(128)S(6)} %select_n.156, s32[]{:T(128)} %constant.105.clone.1, s32[]{:T(128)} %constant.105.clone.1) | dynamic-update-slice | bytes 1048580 | tf_op jit(solution)/shard_map/dynamic_update_slice | solution.py:20
  300.0 42.9 %dynamic_update_slice.55 = f32[1024,256,8]{0,2,1:T(8,128)} dynamic-update-slice(f32[1024,256,8]{0,2,1:T(8,128)} %dynamic_update_slice.54, f32[64,256,8]{0,2,1:T(8,128)S(1)} %copy.95, s32[]{:T(128)S(6)} %select_n.158, s32[]{:T(128)} %constant.105.clone.1, s32[]{:T(128)} %constant.105.clone.1) | dynamic-update-slice | bytes 1048580 | tf_op jit(solution)/shard_map/dynamic_update_slice | solution.py:17
  343.4 43.1 %dynamic_update_slice.56 = f32[1024,256,8]{0,2,1:T(8,128)} dynamic-update-slice(f32[1024,256,8]{0,2,1:T(8,128)} %dynamic_update_slice.55, f32[64,256,8]{0,2,1:T(8,128)S(1)} %copy.96, s32[]{:T(128)S(6)} %select_n.160, s32[]{:T(128)} %constant.105.clone.1, s32[]{:T(128)} %constant.105.clone.1) | dynamic-update-slice | bytes 1048580 | tf_op jit(solution)/shard_map/dynamic_update_slice | solution.py:20
  388.0 8.3 %dynamic_update_slice.57 = f32[1024,256,8]{0,2,1:T(8,128)} dynamic-update-slice(f32[1024,256,8]{0,2,1:T(8,128)} %dynamic_update_slice.56, f32[64,256,8]{0,2,1:T(8,128)S(1)} %copy.97, s32[]{:T(128)S(6)} %select_n.162, s32[]{:T(128)} %constant.105.clone.1, s32[]{:T(128)} %constant.105.clone.1) | dynamic-update-slice | bytes 1048580 | tf_op jit(solution)/shard_map/dynamic_update_slice | solution.py:17
  397.8 8.4 %dynamic_update_slice.58 = f32[1024,256,8]{0,2,1:T(8,128)} dynamic-update-slice(f32[1024,256,8]{0,2,1:T(8,128)} %dynamic_update_slice.57, f32[64,256,8]{0,2,1:T(8,128)S(1)} %copy.98, s32[]{:T(128)S(6)} %select_n.164, s32[]{:T(128)} %constant.105.clone.1, s32[]{:T(128)} %constant.105.clone.1) | dynamic-update-slice | bytes 1048580 | tf_op jit(solution)/shard_map/dynamic_update_slice | solution.py:20
  407.6 42.9 %dynamic_update_slice.59 = f32[1024,256,8]{0,2,1:T(8,128)} dynamic-update-slice(f32[1024,256,8]{0,2,1:T(8,128)} %dynamic_update_slice.58, f32[64,256,8]{0,2,1:T(8,128)S(1)} %copy.99, s32[]{:T(128)S(6)} %select_n.166, s32[]{:T(128)} %constant.105.clone.1, s32[]{:T(128)} %constant.105.clone.1) | dynamic-update-slice | bytes 1048580 | tf_op jit(solution)/shard_map/dynamic_update_slice | solution.py:17
  451.0 43.0 %dynamic_update_slice.60 = f32[1024,256,8]{0,2,1:T(8,128)} dynamic-update-slice(f32[1024,256,8]{0,2,1:T(8,128)} %dynamic_update_slice.59, f32[64,256,8]{0,2,1:T(8,128)S(1)} %copy.100, s32[]{:T(128)S(6)} %select_n.168, s32[]{:T(128)} %constant.105.clone.1, s32[]{:T(128)} %constant.105.clone.1) | dynamic-update-slice | bytes 1048580 | tf_op jit(solution)/shard_map/dynamic_update_slice | solution.py:20
  495.4 8.3 %dynamic_update_slice.61 = f32[1024,256,8]{0,2,1:T(8,128)} dynamic-update-slice(f32[1024,256,8]{0,2,1:T(8,128)} %dynamic_update_slice.60, f32[64,256,8]{0,2,1:T(8,128)S(1)} %copy.101, s32[]{:T(128)S(6)} %select_n.170, s32[]{:T(128)} %constant.105.clone.1, s32[]{:T(128)} %constant.105.clone.1) | dynamic-update-slice | bytes 1048580 | tf_op jit(solution)/shard_map/dynamic_update_slice | solution.py:17
  505.3 8.4 %dynamic_update_slice.62 = f32[1024,256,8]{0,2,1:T(8,128)} dynamic-update-slice(f32[1024,256,8]{0,2,1:T(8,128)} %dynamic_update_slice.61, f32[64,256,8]{0,2,1:T(8,128)S(1)} %copy.102, s32[]{:T(128)S(6)} %select_n.172, s32[]{:T(128)} %constant.105.clone.1, s32[]{:T(128)} %constant.105.clone.1) | dynamic-update-slice | bytes 1048580 | tf_op jit(solution)/shard_map/dynamic_update_slice | solution.py:20
  513.6 41.5 %collective-permute-start.14 = (f32[64,256,8]{1,2,0:T(8,128)}, f32[64,256,8]{1,2,0:T(8,128)S(1)}, u32[]{:S(2)}, u32[]{:S(2)}) collective-permute-start(f32[64,256,8]{1,2,0:T(8,128)} %collective-permute-done.12), channel_id=1, source_target_pairs={{0,32},{32,64},{64,96},{96,128},{128,160},{160,192},{192,224},{224... | collective-permute-start | bytes 1572872 | tf_op jit(solution)/shard_map/ppermute | solution.py:16
  564.7 42.9 %dynamic_update_slice.63 = f32[1024,256,8]{0,2,1:T(8,128)} dynamic-update-slice(f32[1024,256,8]{0,2,1:T(8,128)} %dynamic_update_slice.62, f32[64,256,8]{0,2,1:T(8,128)S(1)} %copy.103, s32[]{:T(128)S(6)} %select_n.174, s32[]{:T(128)} %constant.105.clone.1, s32[]{:T(128)} %constant.105.clone.1) | dynamic-update-slice | bytes 1048580 | tf_op jit(solution)/shard_map/dynamic_update_slice | solution.py:17
  607.6 30.5 %cosine_bitcast_fusion = (f32[256,8,1024]{2,1,0:T(8,128)S(1)}, f32[256,8,1024]{2,1,0:T(8,128)S(1)}) fusion(f32[1024,256,8]{0,2,1:T(8,128)} %dynamic_update_slice.63), kind=kLoop, calls=%fused_computation.5 | loop fusion | bytes 25165824 | tf_op jit(solution)/shard_map/dot_general | solution.py:80
  638.1 9.3 %fusion = f32[64,256,8]{1,0,2:T(8,128)S(1)} fusion(f32[256,8,1024]{2,1,0:T(8,128)S(1)} %get-tuple-element.6, s32[64]{0:T(128)S(1)} %bitcast_add_fusion), kind=kOutput, calls=%fused_computation | convolution fusion | flops 1610678272 | bytes 8913152 | tf_op jit(solution)/shard_map/dot_general | solution.py:86
  647.5 9.5 %fusion.2 = f32[64,256,8]{1,0,2:T(8,128)S(1)} fusion(f32[256,8,1024]{2,1,0:T(8,128)S(1)} %get-tuple-element.5, s32[64]{0:T(128)S(1)} %bitcast_add_fusion), kind=kOutput, calls=%fused_computation.2 | convolution fusion | flops 1610678272 | bytes 8913152 | tf_op jit(solution)/shard_map/dot_general | solution.py:80
  666.1 72.5 %all_to_all.30 = f32[128,256,8]{0,2,1:T(8,128)S(1)} all-to-all(f32[128,256,8]{0,2,1:T(8,128)S(1)} %copy.112), channel_id=1, replica_groups=mesh['tile'=16,'depth'=32] {'depth'}, dimensions={1} | all-to-all | bytes 2097152 | tf_op jit(solution)/shard_map/all_to_all | solution.py:29
  (98 shorter events, 81.2 us)
Async XLA Ops:
  0.0 1.0 copy-start
  0.0 21.7 %copy-start.2 = (f32[64,256,8]{1,2,0:T(8,128)S(1)}, f32[64,256,8]{1,2,0:T(8,128)}, u32[]{:S(2)}) copy-start(f32[64,256,8]{1,2,0:T(8,128)} %param.7) | copy-start | bytes 1572868
  4.4 168.6 %copy-start.14 = (s32[64]{0:T(128)S(1)}, s32[64]{0:T(128)}, u32[]{:S(2)}) copy-start(s32[64]{0:T(128)} %param.6) | copy-start | bytes 772
  4.4 168.6 %copy-start.15 = (s32[64,1]{0,1:T(1,128)S(1)}, s32[64,1]{0,1:T(1,128)}, u32[]{:S(2)}) copy-start(s32[64,1]{0,1:T(1,128)} %param.5) | copy-start | bytes 772
  5.7 549.3 %all-to-all-start = ((f32[128,8,256]{0,1,2:T(8,128)}), f32[128,8,256]{0,1,2:T(8,128)S(1)}, u32[]{:S(2)}, u32[]{:S(2)}) async-start(f32[128,8,256]{0,1,2:T(8,128)} %copy.82), calls=%async_computation | async-start | bytes 2097152 | tf_op jit(solution)/shard_map/all_to_all | solution.py:29
  21.7 15.2 %collective-permute-start = (f32[64,256,8]{1,2,0:T(8,128)S(1)}, f32[64,256,8]{1,2,0:T(8,128)}, u32[]{:S(2)}, u32[]{:S(2)}) collective-permute-start(f32[64,256,8]{1,2,0:T(8,128)S(1)} %copy-done.2), channel_id=1, source_target_pairs={{0,32},{32,64},{64,96},{96,128},{128,160},{160,192},{192,224},{224... | collective-permute-start | bytes 1572872 | tf_op jit(solution)/shard_map/ppermute | solution.py:16
  23.6 18.7 %collective-permute-start.1 = (f32[64,256,8]{1,2,0:T(8,128)S(1)}, f32[64,256,8]{1,2,0:T(8,128)S(1)}, u32[]{:S(2)}, u32[]{:S(2)}) collective-permute-start(f32[64,256,8]{1,2,0:T(8,128)S(1)} %copy-done.2), channel_id=1, source_target_pairs={{0,480},{32,0},{64,32},{96,64},{128,96},{160,128},{192,160},{224,1... | collective-permute-start | bytes 1572872 | tf_op jit(solution)/shard_map/ppermute | solution.py:19
  36.9 16.0 %collective-permute-start.2 = (f32[64,256,8]{1,2,0:T(8,128)}, f32[64,256,8]{1,2,0:T(8,128)}, u32[]{:S(2)}, u32[]{:S(2)}) collective-permute-start(f32[64,256,8]{1,2,0:T(8,128)} %collective-permute-done), channel_id=1, source_target_pairs={{0,32},{32,64},{64,96},{96,128},{128,160},{160,192},{192,224},{224... | collective-permute-start | bytes 1572872 | tf_op jit(solution)/shard_map/ppermute | solution.py:16
  42.3 66.4 %copy-start.3 = (f32[64,256,8]{1,2,0:T(8,128)}, f32[64,256,8]{1,2,0:T(8,128)S(1)}, u32[]{:S(2)}) copy-start(f32[64,256,8]{1,2,0:T(8,128)S(1)} %collective-permute-done.1) | copy-start | bytes 1572868
  42.3 18.0 %collective-permute-start.3 = (f32[64,256,8]{1,2,0:T(8,128)S(1)}, f32[64,256,8]{1,2,0:T(8,128)}, u32[]{:S(2)}, u32[]{:S(2)}) collective-permute-start(f32[64,256,8]{1,2,0:T(8,128)S(1)} %collective-permute-done.1), channel_id=1, source_target_pairs={{0,480},{32,0},{64,32},{96,64},{128,96},{160,128},{192,160},{224,1... | collective-permute-start | bytes 1572872 | tf_op jit(solution)/shard_map/ppermute | solution.py:19
  53.0 17.2 %collective-permute-start.4 = (f32[64,256,8]{1,2,0:T(8,128)}, f32[64,256,8]{1,2,0:T(8,128)S(1)}, u32[]{:S(2)}, u32[]{:S(2)}) collective-permute-start(f32[64,256,8]{1,2,0:T(8,128)} %collective-permute-done.2), channel_id=1, source_target_pairs={{0,32},{32,64},{64,96},{96,128},{128,160},{160,192},{192,224},{224... | collective-permute-start | bytes 1572872 | tf_op jit(solution)/shard_map/ppermute | solution.py:16
  60.4 17.1 %collective-permute-start.5 = (f32[64,256,8]{1,2,0:T(8,128)}, f32[64,256,8]{1,2,0:T(8,128)S(1)}, u32[]{:S(2)}, u32[]{:S(2)}) collective-permute-start(f32[64,256,8]{1,2,0:T(8,128)} %collective-permute-done.3), channel_id=1, source_target_pairs={{0,480},{32,0},{64,32},{96,64},{128,96},{160,128},{192,160},{224,1... | collective-permute-start | bytes 1572872 | tf_op jit(solution)/shard_map/ppermute | solution.py:19
  70.2 55.0 %copy-start.5 = (f32[64,256,8]{1,2,0:T(8,128)}, f32[64,256,8]{1,2,0:T(8,128)S(1)}, u32[]{:S(2)}) copy-start(f32[64,256,8]{1,2,0:T(8,128)S(1)} %collective-permute-done.4) | copy-start | bytes 1572868
  70.2 15.9 %collective-permute-start.6 = (f32[64,256,8]{1,2,0:T(8,128)S(1)}, f32[64,256,8]{1,2,0:T(8,128)S(1)}, u32[]{:S(2)}, u32[]{:S(2)}) collective-permute-start(f32[64,256,8]{1,2,0:T(8,128)S(1)} %collective-permute-done.4), channel_id=1, source_target_pairs={{0,32},{32,64},{64,96},{96,128},{128,160},{160,192},{192,224},{224... | collective-permute-start | bytes 1572872 | tf_op jit(solution)/shard_map/ppermute | solution.py:16
  77.5 47.7 %copy-start.7 = (f32[64,256,8]{1,2,0:T(8,128)}, f32[64,256,8]{1,2,0:T(8,128)S(1)}, u32[]{:S(2)}) copy-start(f32[64,256,8]{1,2,0:T(8,128)S(1)} %collective-permute-done.5) | copy-start | bytes 1572868
  77.5 16.0 %collective-permute-start.7 = (f32[64,256,8]{1,2,0:T(8,128)S(1)}, f32[64,256,8]{1,2,0:T(8,128)S(1)}, u32[]{:S(2)}, u32[]{:S(2)}) collective-permute-start(f32[64,256,8]{1,2,0:T(8,128)S(1)} %collective-permute-done.5), channel_id=1, source_target_pairs={{0,480},{32,0},{64,32},{96,64},{128,96},{160,128},{192,160},{224,1... | collective-permute-start | bytes 1572872 | tf_op jit(solution)/shard_map/ppermute | solution.py:19
  86.1 37.1 %copy-start.8 = (f32[64,256,8]{1,2,0:T(8,128)}, f32[64,256,8]{1,2,0:T(8,128)S(1)}, u32[]{:S(2)}) copy-start(f32[64,256,8]{1,2,0:T(8,128)S(1)} %collective-permute-done.6) | copy-start | bytes 1572868
  86.1 15.2 %collective-permute-start.8 = (f32[64,256,8]{1,2,0:T(8,128)S(1)}, f32[64,256,8]{1,2,0:T(8,128)S(1)}, u32[]{:S(2)}, u32[]{:S(2)}) collective-permute-start(f32[64,256,8]{1,2,0:T(8,128)S(1)} %collective-permute-done.6), channel_id=1, source_target_pairs={{0,32},{32,64},{64,96},{96,128},{128,160},{160,192},{192,224},{224... | collective-permute-start | bytes 1572872 | tf_op jit(solution)/shard_map/ppermute | solution.py:16
  93.5 31.6 %copy-start.9 = (f32[64,256,8]{1,2,0:T(8,128)}, f32[64,256,8]{1,2,0:T(8,128)S(1)}, u32[]{:S(2)}) copy-start(f32[64,256,8]{1,2,0:T(8,128)S(1)} %collective-permute-done.7) | copy-start | bytes 1572868
  93.5 15.2 %collective-permute-start.9 = (f32[64,256,8]{1,2,0:T(8,128)S(1)}, f32[64,256,8]{1,2,0:T(8,128)S(1)}, u32[]{:S(2)}, u32[]{:S(2)}) collective-permute-start(f32[64,256,8]{1,2,0:T(8,128)S(1)} %collective-permute-done.7), channel_id=1, source_target_pairs={{0,480},{32,0},{64,32},{96,64},{128,96},{160,128},{192,160},{224,1... | collective-permute-start | bytes 1572872 | tf_op jit(solution)/shard_map/ppermute | solution.py:19
  101.3 23.8 %copy-start.11 = (f32[64,256,8]{1,2,0:T(8,128)}, f32[64,256,8]{1,2,0:T(8,128)S(1)}, u32[]{:S(2)}) copy-start(f32[64,256,8]{1,2,0:T(8,128)S(1)} %collective-permute-done.8) | copy-start | bytes 1572868
  101.3 14.3 %collective-permute-start.10 = (f32[64,256,8]{1,2,0:T(8,128)S(1)}, f32[64,256,8]{1,2,0:T(8,128)}, u32[]{:S(2)}, u32[]{:S(2)}) collective-permute-start(f32[64,256,8]{1,2,0:T(8,128)S(1)} %collective-permute-done.8), channel_id=1, source_target_pairs={{0,32},{32,64},{64,96},{96,128},{128,160},{160,192},{192,224},{224... | collective-permute-start | bytes 1572872 | tf_op jit(solution)/shard_map/ppermute | solution.py:16
  108.7 16.4 %copy-start.12 = (f32[64,256,8]{1,2,0:T(8,128)}, f32[64,256,8]{1,2,0:T(8,128)S(1)}, u32[]{:S(2)}) copy-start(f32[64,256,8]{1,2,0:T(8,128)S(1)} %collective-permute-done.9) | copy-start | bytes 1572868
  108.7 14.4 %collective-permute-start.11 = (f32[64,256,8]{1,2,0:T(8,128)S(1)}, f32[64,256,8]{1,2,0:T(8,128)S(1)}, u32[]{:S(2)}, u32[]{:S(2)}) collective-permute-start(f32[64,256,8]{1,2,0:T(8,128)S(1)} %collective-permute-done.9), channel_id=1, source_target_pairs={{0,480},{32,0},{64,32},{96,64},{128,96},{160,128},{192,160},{224,1... | collective-permute-start | bytes 1572872 | tf_op jit(solution)/shard_map/ppermute | solution.py:19
  115.6 378.4 %collective-permute-start.12 = (f32[64,256,8]{1,2,0:T(8,128)}, f32[64,256,8]{1,2,0:T(8,128)}, u32[]{:S(2)}, u32[]{:S(2)}) collective-permute-start(f32[64,256,8]{1,2,0:T(8,128)} %collective-permute-done.10), channel_id=1, source_target_pairs={{0,32},{32,64},{64,96},{96,128},{128,160},{160,192},{192,224},{224... | collective-permute-start | bytes 1572872 | tf_op jit(solution)/shard_map/ppermute | solution.py:16
  123.2 380.6 %collective-permute-start.13 = (f32[64,256,8]{1,2,0:T(8,128)S(1)}, f32[64,256,8]{1,2,0:T(8,128)}, u32[]{:S(2)}, u32[]{:S(2)}) collective-permute-start(f32[64,256,8]{1,2,0:T(8,128)S(1)} %collective-permute-done.11), channel_id=1, source_target_pairs={{0,480},{32,0},{64,32},{96,64},{128,96},{160,128},{192,160},{224,1... | collective-permute-start | bytes 1572872 | tf_op jit(solution)/shard_map/ppermute | solution.py:19
  125.6 56.5 %copy-start.4 = (f32[64,256,8]{1,2,0:T(8,128)S(1)}, f32[64,256,8]{1,2,0:T(8,128)}, u32[]{:S(2)}) copy-start(f32[64,256,8]{1,2,0:T(8,128)} %copy-done.3) | copy-start | bytes 1572868
  182.6 97.2 %copy-start.6 = (f32[64,256,8]{1,2,0:T(8,128)S(1)}, f32[64,256,8]{1,2,0:T(8,128)}, u32[]{:S(2)}) copy-start(f32[64,256,8]{1,2,0:T(8,128)} %copy-done.5) | copy-start | bytes 1572868
  280.3 62.6 %copy-start.10 = (f32[64,256,8]{1,2,0:T(8,128)S(1)}, f32[64,256,8]{1,2,0:T(8,128)}, u32[]{:S(2)}) copy-start(f32[64,256,8]{1,2,0:T(8,128)} %copy-done.9) | copy-start | bytes 1572868
  513.6 50.6 %collective-permute-start.14 = (f32[64,256,8]{1,2,0:T(8,128)}, f32[64,256,8]{1,2,0:T(8,128)S(1)}, u32[]{:S(2)}, u32[]{:S(2)}) collective-permute-start(f32[64,256,8]{1,2,0:T(8,128)} %collective-permute-done.12), channel_id=1, source_target_pairs={{0,32},{32,64},{64,96},{96,128},{128,160},{160,192},{192,224},{224... | collective-permute-start | bytes 1572872 | tf_op jit(solution)/shard_map/ppermute | solution.py:16
  638.1 18.8 %copy-start.13 = (f32[64,8,256]{2,1,0:T(8,128)S(1)}, f32[64,8,256]{2,1,0:T(8,128)}, u32[]{:S(2)}) copy-start(f32[64,8,256]{2,1,0:T(8,128)} %fusion.33) | copy-start | bytes 1572868
  738.7 8.5 %copy-start.1 = (f32[64,8,256]{2,1,0:T(8,128)S(1)}, f32[64,8,256]{2,1,0:T(8,128)}, u32[]{:S(2)}) copy-start(f32[64,8,256]{2,1,0:T(8,128)} %param.4) | copy-start | bytes 1572868
